TPU v7x, 128 devices: a whole 4x4x4 slice. The times are simulated.
128 devices in a mesh: row: 16 (over x, y_lo, core), col: 8 (over z, y_hi).
Axes of the slice: x: 4, y: 4 (y_hi: 2, y_lo: 2; y = y_hi * 2 + y_lo), z: 4, core: 2. Of those that a mesh axis runs over, the one named last changes fastest.
Arguments:
- upper_s: float32 [2, 4096, 4, 2048], P(None, 'row', None, 'col')
- upper_t: float32 [2, 4096, 4, 2048], P(None, 'row', None, 'col')
- left_vectors: float32 [2, 4096, 4, 2048], P(None, 'row', None, 'col'), may hold values from -6 to 6
- right_vectors: float32 [2, 4096, 4, 2048], P(None, 'row', None, 'col'), may hold values from -6 to 6
- window_starts: int32 [3, 16], replicated, may hold values from 0 to 31, as said below
- selection: int32 [3, 16, 256], replicated, may hold values 0 or 1
- window_factors: float32 [3, 16, 2, 256, 256], P(None, 'row')
Outputs:
- new_s: float32 [2, 4096, 4, 2048], P(None, 'row', None, 'col')
- new_t: float32 [2, 4096, 4, 2048], P(None, 'row', None, 'col')
- new_left: float32 [2, 4096, 4, 2048], P(None, 'row', None, 'col')
- new_right: float32 [2, 4096, 4, 2048], P(None, 'row', None, 'col')
Inputs may be any that keep to these rules, and one draw needn't show every extreme that they name: `window_starts`: within each round the 16 block numbers are distinct.
All inputs are finite; a program needn't handle non-finite values.
Results may differ from a plain program's by a relative error of at most 0.0001.
Values sent between devices are 32-bit elements; how exact they have to be, the bound alone decides.
A program may use at most 128 MiB of HBM per device.

v0:
```python
import functools

import jax
import jax.numpy as jnp
from jax import lax
from jax.experimental import pallas as pl
from jax.experimental.pallas import tpu as pltpu
from jax.sharding import PartitionSpec as P

F32, BF = jnp.float32, jnp.bfloat16
MESH = pl.DeviceIdType.MESH
ANY = pl.BlockSpec(memory_space=pl.ANY)
VM = pl.BlockSpec(memory_space=pltpu.VMEM)
SM = pl.BlockSpec(memory_space=pltpu.SMEM)
W = 256
NQ, NC, NB, NK = 8, 8, 4, 3


def split(x):
    hi = x.astype(BF)
    return hi, (x - hi.astype(F32)).astype(BF)


def mm(a, b):
    d = functools.partial(jnp.dot, preferred_element_type=F32)
    return d(a[0], b[0]) + (d(a[0], b[1]) + d(a[1], b[0]))


def permute_kernel(starts, sel, wf, send, inv):
    r, c = lax.axis_index("row"), lax.axis_index("col")
    lane = lax.broadcasted_iota(jnp.int32, (32, W), 1)
    pos = lax.broadcasted_iota(jnp.int32, (32, W), 0) + c * 32
    pos1 = lax.broadcasted_iota(jnp.int32, (32, 1), 0) + c * 32
    win = lax.broadcasted_iota(jnp.int32, (16, 16), 0)
    win_l = lax.broadcasted_iota(jnp.int32, (16, 16), 1)
    blk = lax.broadcasted_iota(jnp.int32, (16, 32), 1)
    win_b = lax.broadcasted_iota(jnp.int32, (16, 32), 0)
    for k in range(NK):
        flags = jnp.broadcast_to(sel[k, pl.ds(r, 1), :], (32, W))
        earlier = jnp.sum(jnp.where(lane < pos, flags, 0), axis=1, keepdims=True)
        own = jnp.sum(jnp.where(lane == pos, flags, 0), axis=1, keepdims=True)
        chosen = jnp.sum(flags, axis=1, keepdims=True)
        target = jnp.where(own == 1, earlier, chosen + pos1 - earlier)
        onehot = jnp.where(lane == target, 1.0, 0.0).astype(BF)
        for x in range(2):
            f = wf[k, 0, x]
            hi = f.astype(BF)
            rest = f - hi.astype(F32)
            mid = rest.astype(BF)
            lo = (rest - mid.astype(F32)).astype(BF)
            d = functools.partial(jnp.dot, preferred_element_type=F32)
            rows = (d(onehot, hi) + d(onehot, mid)) + d(onehot, lo)
            for q in range(NQ):
                send[q, x, k] = rows[(q // 2) * 8:(q // 2) * 8 + 8, (q % 2) * 128:(q % 2) * 128 + 128]
        st = jnp.broadcast_to(starts[k:k + 1, :], (16, 16))
        col = jnp.sum(jnp.where(win == win_l, st, 0), axis=1, keepdims=True)
        inv[k:k + 1, :] = 16 + jnp.sum(jnp.where(col == blk, win_b - 16, 0), axis=0, keepdims=True)


def task_chip(b, x, c):
    xx = (c // 4 + x + 2 * (b % 2)) % 4
    flip = b // 2
    y = (flip + (1 - x) * ((c // 2) % 2)) % 2
    return xx * 2 + y


def comm_kernel(inv, send_a, colf, rowl, recv_a, send_b, recv_b, combo,
                a_send, a_recv, b_send, b_recv, c_send, c_recv, d_send, d_recv, e_send, e_recv):
    r, c = lax.axis_index("row"), lax.axis_index("col")
    q, s = r // 2, r % 2
    rt, lt = c * 4 + q // 2, q % 2
    bx = (q // 2 + 4 - c // 4) % 4
    task_x = bx % 2
    is_task = task_x == s
    task_b = bx // 2 + 2 * jnp.where(task_x == 0, (q + c // 2) % 2, q % 2)

    def put(src, dst, ssem, rsem, rr, cc):
        me = jnp.logical_and(rr == r, cc == c)

        @pl.when(me)
        def _():
            pltpu.make_async_copy(src, dst, rsem).start()

        @pl.when(jnp.logical_not(me))
        def _():
            pltpu.make_async_remote_copy(src, dst, ssem, rsem, device_id=(rr, cc), device_id_type=MESH).start()

    def wait_for(ref, sem):
        pltpu.make_async_copy(ref, ref, sem).wait()

    def spread(i, _):
        rr = (r + i) % 16
        put(send_a.at[rr // 2, rr % 2], recv_a.at[r], a_send, a_recv, rr, c)
        return 0

    lax.fori_loop(0, 16, spread, 0)
    ident = jnp.where(
        lax.broadcasted_iota(jnp.int32, (8, 128), 0) + rt * 8
        == lax.broadcasted_iota(jnp.int32, (8, 128), 1) + lt * 128, 1.0, 0.0).astype(F32)
    for k in range(NK):
        recv_a[16, k] = ident
    wait_for(recv_a.at[pl.ds(0, 16)], a_recv)

    def pick(i, _):
        for k in range(NK):
            send_b[i, k] = recv_a[inv[k, i], k]
        return 0

    lax.fori_loop(0, 32, pick, 0)

    def gather(i, _):
        cc, b = (c + i // NB) % NC, i % NB
        put(send_b.at[cc + 8 * b],
            recv_b.at[:, pl.ds(pl.multiple_of(rt * 8, 8), 8), pl.ds(pl.multiple_of(lt * 128, 128), 128)],
            b_send, b_recv, task_chip(b, s, cc) * 2 + s, cc)
        return 0

    lax.fori_loop(0, 32, gather, 0)

    @pl.when(is_task)
    def _():
        wait_for(recv_b, b_recv)
        combo[...] = mm(split(mm(split(recv_b[0]), split(recv_b[1]))), split(recv_b[2]))
        slot = task_x * NB + task_b

        def tell(i, _):
            rr = (r + i) % 16
            half = pl.ds(pl.multiple_of((rr % 2) * 128, 128), 128)
            put(combo.at[half], colf.at[slot, half], c_send, c_recv.at[slot], rr, c)
            return 0

        lax.fori_loop(0, 16, tell, 0)

        @pl.when(task_x == 0)
        def _():
            def tell_row(i, _):
                put(combo, rowl.at[task_b // 2], d_send, d_recv, c + 8 * (task_b % 2), (c + i) % NC)
                return 0

            lax.fori_loop(0, NC, tell_row, 0)

    half = pl.ds(pl.multiple_of(s * 128, 128), 128)
    other = pl.ds(pl.multiple_of((1 - s) * 128, 128), 128)

    def forward(i, _):
        wait_for(colf.at[i, half], c_recv.at[i])
        pltpu.make_async_remote_copy(colf.at[i, half], colf.at[i, half], e_send, e_recv,
                                     device_id=(r + 1 - 2 * s, c), device_id_type=MESH).start()
        return 0

    lax.fori_loop(0, 8, forward, 0)
    wait_for(rowl, d_recv)
    wait_for(colf.at[:, other], e_recv)
    wait_for(colf.at[:, half], e_send)
    wait_for(recv_a.at[pl.ds(0, 15)], a_send)

    @pl.when(is_task)
    def _():
        wait_for(send_b.at[pl.ds(0, 31)], b_send)
        wait_for(colf.at[:, pl.ds(0, 240)], c_send)

        @pl.when(task_x == 0)
        def _():
            mine = c + 8 * (task_b % 2) == r

            @pl.when(mine)
            def _():
                wait_for(colf.at[pl.ds(0, 7)], d_send)

            @pl.when(jnp.logical_not(mine))
            def _():
                wait_for(colf, d_send)

    @pl.when(jnp.logical_not(is_task))
    def _():
        wait_for(send_b, b_send)


def comm_call(inv, send_a):
    dma = pltpu.SemaphoreType.DMA
    return pl.pallas_call(
        comm_kernel,
        out_shape=[jax.ShapeDtypeStruct((2 * NB, W, W), F32), jax.ShapeDtypeStruct((2, W, W), F32)],
        in_specs=[SM, VM],
        out_specs=[ANY, ANY],
        scratch_shapes=[
            pltpu.VMEM((17, NK, 8, 128), F32), pltpu.VMEM((32, NK, 8, 128), F32),
            pltpu.VMEM((NK, W, W), F32), pltpu.VMEM((W, W), F32),
            dma, dma, dma, dma, dma, dma((8,)), dma, dma, dma, dma,
        ],
        compiler_params=pltpu.CompilerParams(has_side_effects=True, vmem_limit_bytes=12 * 1024 * 1024),
        name="comm",
    )(inv, send_a)


def permute_call(starts, sel, wf):
    return pl.pallas_call(
        permute_kernel,
        out_shape=[jax.ShapeDtypeStruct((NQ, 2, NK, 8, 128), F32), jax.ShapeDtypeStruct((NK, 32), jnp.int32)],
        in_specs=[VM, VM, VM],
        out_specs=[VM, VM],
        name="permute",
    )(starts, sel, wf)


def apply_kernel(s, t, q, z, colf, rowl, os, ot, oq, oz, buf, obuf, ch, cl, rh, rl, in_sem, out_sem):
    br, w, bc, _ = s.shape
    mats, outs = (s, t, q, z), (os, ot, oq, oz)
    def load(m, a, b):
        return pltpu.make_async_copy(mats[m].at[a, :, b, :], buf.at[m, a * bc + b], in_sem.at[m, a * bc + b])
    def store(m, a, b):
        return pltpu.make_async_copy(obuf.at[m, a * bc + b], outs[m].at[a, :, b, :], out_sem.at[m, a * bc + b])
    for a in range(br):
        for b in range(bc):
            for m in range(4):
                load(m, a, b).start()
    for a in range(br):
        h, l = split(rowl[a].T)
        rh[a], rl[a] = h, l
    def cs(i, _):
        h, l = split(colf[i])
        ch[i], cl[i] = h, l
        return 0
    lax.fori_loop(0, 2 * bc, cs, 0)
    def step(i, _):
        a, b = i // bc, i % bc
        for m in range(4):
            load(m, a, b).wait()
        left = (ch[b], cl[b])
        right = (ch[bc + b], cl[bc + b])
        row = (rh[a], rl[a])
        for m in range(4):
            x = split(buf[m, i])
            y = mm(x, left if m == 2 else right)
            if m < 2:
                y = mm(row, split(y))
            obuf[m, i] = y
            store(m, a, b).start()
        return 0
    lax.fori_loop(0, br * bc, step, 0)
    for a in range(br):
        for b in range(bc):
            for m in range(4):
                store(m, a, b).wait()

def apply_call(s, t, q, z, colf, rowl):
    br, w, bc, _ = s.shape
    return pl.pallas_call(
        apply_kernel,
        out_shape=[jax.ShapeDtypeStruct(s.shape, F32)] * 4,
        in_specs=[ANY] * 4 + [VM, VM],
        out_specs=[ANY] * 4,
        scratch_shapes=[
            pltpu.VMEM((4, br * bc, w, w), F32), pltpu.VMEM((4, br * bc, w, w), F32),
            pltpu.VMEM((2 * bc, w, w), BF), pltpu.VMEM((2 * bc, w, w), BF),
            pltpu.VMEM((br, w, w), BF), pltpu.VMEM((br, w, w), BF),
            pltpu.SemaphoreType.DMA((4, br * bc)), pltpu.SemaphoreType.DMA((4, br * bc)),
        ],
        compiler_params=pltpu.CompilerParams(vmem_limit_bytes=40 * 1024 * 1024),
        name="apply",
    )(s, t, q, z, colf, rowl)


def shards(s, t, q, z, starts, sel, wf):
    send, inv = permute_call(starts, sel, wf)
    colf, rowl = comm_call(inv, send)
    return apply_call(s, t, q, z, colf, rowl)


def solution(mesh):
    spec = P(None, "row", None, "col")
    return jax.shard_map(
        shards,
        mesh=mesh,
        in_specs=(spec,) * 4 + (P(), P(), P(None, "row")),
        out_specs=(spec,) * 4,
        check_vma=False,
    )
```

profile of v0, /device:TPU:25, one launch (start us, length us, event | category | flops | bytes accessed | tf_op | source)
XLA Modules:
  0.0 94.4 jit_solution(10770303323795776397)
XLA Ops:
  0.6 2.8 %permute.1 = (f32[8,2,3,8,128]{4,3,2,1,0:T(8,128)}, s32[3,32]{1,0:T(4,128)}) custom-call(s32[3,16]{1,0:T(4,128)} %starts.1, s32[3,16,256]{2,1,0:T(8,128)} %sel.1, f32[3,1,2,256,256]{4,3,2,1,0:T(8,128)} %wf.1), custom_call_target="tpu_custom_call" | custom-call | tf_op jit(solution)/shard_map/permute/pallas_call | solution.py:197
  3.4 0.0 copy-start.4
  3.4 0.9 copy-done.4
  4.3 0.0 copy-start.5
  4.3 0.7 copy-done.5
  5.0 59.7 %comm.1 = (f32[8,256,256]{2,1,0:T(8,128)S(1)}, f32[2,256,256]{2,1,0:T(8,128)S(1)}) custom-call(s32[3,32]{1,0:T(4,128)S(1)} %copy-done.5, f32[8,2,3,8,128]{4,3,2,1,0:T(8,128)S(1)} %copy-done.4), custom_call_target="tpu_custom_call" | custom-call | tf_op jit(solution)/shard_map/comm/pallas_call | solution.py:181
  64.7 0.0 copy-start
  64.7 1.6 %copy-done = f32[2,256,4,256]{3,2,1,0:T(4,128)S(1)} copy-done((f32[2,256,4,256]{3,2,1,0:T(4,128)S(1)}, f32[2,256,4,256]{3,2,1,0:T(4,128)}, u32[]{:S(2)}) %copy-start) | copy-done | bytes 2097176
  66.3 0.0 copy-start.1
  66.3 1.6 %copy-done.1 = f32[2,256,4,256]{3,2,1,0:T(4,128)S(1)} copy-done((f32[2,256,4,256]{3,2,1,0:T(4,128)S(1)}, f32[2,256,4,256]{3,2,1,0:T(4,128)}, u32[]{:S(2)}) %copy-start.1) | copy-done | bytes 2097176
  67.9 0.0 copy-start.2
  67.9 1.6 %copy-done.2 = f32[2,256,4,256]{3,2,1,0:T(4,128)S(1)} copy-done((f32[2,256,4,256]{3,2,1,0:T(4,128)S(1)}, f32[2,256,4,256]{3,2,1,0:T(4,128)}, u32[]{:S(2)}) %copy-start.2) | copy-done | bytes 2097176
  69.5 0.0 copy-start.3
  69.5 1.6 %copy-done.3 = f32[2,256,4,256]{3,2,1,0:T(4,128)S(1)} copy-done((f32[2,256,4,256]{3,2,1,0:T(4,128)S(1)}, f32[2,256,4,256]{3,2,1,0:T(4,128)}, u32[]{:S(2)}) %copy-start.3) | copy-done | bytes 2097176
  71.0 23.4 %apply.1 = (f32[2,256,4,256]{3,2,1,0:T(4,128)}, f32[2,256,4,256]{3,2,1,0:T(4,128)}, f32[2,256,4,256]{3,2,1,0:T(4,128)}, f32[2,256,4,256]{3,2,1,0:T(4,128)}) custom-call(f32[2,256,4,256]{3,2,1,0:T(4,128)S(1)} %copy-done, f32[2,256,4,256]{3,2,1,0:T(4,128)S(1)} %copy-done.1, f32[2,256,4,256]{3,2,1,0:T(4,128)S(1)} %copy-done.2, ...), custom_call_target="tpu_custom_call" | custom-call | tf_op jit(solution)/shard_map/apply/pallas_call | solution.py:248
Async XLA Ops:
  3.4 0.9 copy-start.4
  4.3 0.7 copy-start.5
  64.7 1.6 %copy-start = (f32[2,256,4,256]{3,2,1,0:T(4,128)S(1)}, f32[2,256,4,256]{3,2,1,0:T(4,128)}, u32[]{:S(2)}) copy-start(f32[2,256,4,256]{3,2,1,0:T(4,128)} %s.1) | copy-start | bytes 6291460
  66.3 1.6 %copy-start.1 = (f32[2,256,4,256]{3,2,1,0:T(4,128)S(1)}, f32[2,256,4,256]{3,2,1,0:T(4,128)}, u32[]{:S(2)}) copy-start(f32[2,256,4,256]{3,2,1,0:T(4,128)} %t.1) | copy-start | bytes 6291460
  67.9 1.6 %copy-start.2 = (f32[2,256,4,256]{3,2,1,0:T(4,128)S(1)}, f32[2,256,4,256]{3,2,1,0:T(4,128)}, u32[]{:S(2)}) copy-start(f32[2,256,4,256]{3,2,1,0:T(4,128)} %q.1) | copy-start | bytes 6291460
  69.5 1.6 %copy-start.3 = (f32[2,256,4,256]{3,2,1,0:T(4,128)S(1)}, f32[2,256,4,256]{3,2,1,0:T(4,128)}, u32[]{:S(2)}) copy-start(f32[2,256,4,256]{3,2,1,0:T(4,128)} %z.1) | copy-start | bytes 6291460
where the time goes:
time: 94.7 us; the launch traced here: 94.4 us
  Pallas kernels  85.8 us (91%)
  local copies, waits for them, and re-layouts  7.97 us (8%)
    pallas_call x1, Pallas kernels, comm_call(): pl.pallas_call(comm_kernel, out_shape=[jax.ShapeDtypeStruct((2 * NB, W, W...  59.7 us
    pallas_call x1, Pallas kernels, apply_call(): pl.pallas_call(apply_kernel, out_shape=[jax.ShapeDtypeStruct(s.shape, F32...  23.4 us
    unnamed x12, local copies, waits for them, and re-layouts  7.97 us
    pallas_call x1, Pallas kernels, permute_call(): pl.pallas_call(permute_kernel, out_shape=[jax.ShapeDtypeStruct((NQ, 2, NK...  2.76 us

commit v1 on v0

v1 whole, which is shorter than its diff:
```python
import functools

import jax
import jax.numpy as jnp
from jax import lax
from jax.experimental import pallas as pl
from jax.experimental.pallas import tpu as pltpu
from jax.sharding import PartitionSpec as P

F32, BF = jnp.float32, jnp.bfloat16
MESH = pl.DeviceIdType.MESH
ANY = pl.BlockSpec(memory_space=pl.ANY)
VM = pl.BlockSpec(memory_space=pltpu.VMEM)
W = 256
NQ, NC, NB, NK = 8, 8, 4, 3


def div(a, b):
    return lax.div(a, jnp.int32(b))


def rem(a, b):
    return lax.rem(a, jnp.int32(b))


def split(x):
    hi = x.astype(BF)
    return hi, (x - hi.astype(F32)).astype(BF)


def mm(a, b):
    d = functools.partial(jnp.dot, preferred_element_type=F32)
    return d(a[0], b[0]) + (d(a[0], b[1]) + d(a[1], b[0]))

NT = 2 * NB


def permute_rows(sel, wf, send, r, c):
    lane = lax.broadcasted_iota(jnp.int32, (32, W), 1)
    pos = lax.broadcasted_iota(jnp.int32, (32, W), 0) + c * 32
    pos1 = lax.broadcasted_iota(jnp.int32, (32, 1), 0) + c * 32
    for k in range(NK):
        flags = jnp.broadcast_to(sel[k, pl.ds(r, 1), :], (32, W))
        earlier = jnp.sum(jnp.where(lane < pos, flags, 0), axis=1, keepdims=True)
        own = jnp.sum(jnp.where(lane == pos, flags, 0), axis=1, keepdims=True)
        chosen = jnp.sum(flags, axis=1, keepdims=True)
        target = jnp.where(own == 1, earlier, chosen + pos1 - earlier)
        onehot = jnp.where(lane == target, 1.0, 0.0).astype(BF)
        for x in range(2):
            f = wf[k, x]
            hi = f.astype(BF)
            rest = f - hi.astype(F32)
            mid = rest.astype(BF)
            lo = (rest - mid.astype(F32)).astype(BF)
            d = functools.partial(jnp.dot, preferred_element_type=F32)
            rows = (d(onehot, hi) + d(onehot, mid)) + d(onehot, lo)
            for q in range(NQ):
                send[q, x, k] = rows[(q // 2) * 8:(q // 2) * 8 + 8, (q % 2) * 128:(q % 2) * 128 + 128]


def window_of_block(starts, inv):
    win = lax.broadcasted_iota(jnp.int32, (16, 16), 0)
    win_l = lax.broadcasted_iota(jnp.int32, (16, 16), 1)
    blk = lax.broadcasted_iota(jnp.int32, (16, 128), 1)
    win_b = lax.broadcasted_iota(jnp.int32, (16, 128), 0)
    for k in range(NK):
        st = jnp.broadcast_to(starts[k:k + 1, :], (16, 16))
        col = jnp.sum(jnp.where(win == win_l, st, 0), axis=1, keepdims=True)
        inv[k:k + 1, :] = 16 - jnp.max(jnp.where(col == blk, 16 - win_b, 0), axis=0, keepdims=True)


def task_chip(b, x, c):
    b, c = jnp.int32(b), jnp.int32(c)
    xx = rem(div(c, 4) + x + 2 * rem(b, 2), 4)
    y = rem(div(b, 2) + (1 - x) * rem(div(c, 2), 2), 2)
    return xx * 2 + y


def task_of(xx, y, c):
    bx = rem(xx + 4 - div(c, 4), 4)
    kind = rem(bx, 2)
    return kind, div(bx, 2) + 2 * rem(y + (1 - kind) * rem(div(c, 2), 2), 2)


def comm_kernel(starts_in, sel_in, wf, s_in, t_in, q_in, z_in, rowl, xs, colf, ch, cl,
                starts, sel, wf_v, send_a, inv_v, inv, recv_a, send_b, recv_b, combo, raw,
                ready, s_sem, w_sem, i_sem, raw_sem, x_sem, a_send, a_recv, b_send, b_recv,
                o_send, c_send, c_recv, e_send, e_recv, t_send, d_send, d_recv):
    r, c = lax.axis_index("row"), lax.axis_index("col")
    x, y, h = div(r, 4), rem(div(r, 2), 2), rem(r, 2)
    q, z = div(r, 2), div(c, 2)
    rt, lt = c * 4 + div(q, 2), rem(q, 2)
    kind, task_b = task_of(x, y, c)
    is_task = kind == h

    barrier = pltpu.get_barrier_semaphore()

    def signal(sem, rr, cc):
        pl.semaphore_signal(sem, inc=1, device_id=(rr, cc), device_id_type=MESH)

    for i in (4, 5, 3, 2, 6, 1, 7):
        signal(barrier, r, rem(c + i, NC))
    for i in range(1, 16):
        signal(barrier, rem(r + i, 16), c)

    def remote(src, dst, ssem, rsem, rr, cc):
        pltpu.make_async_remote_copy(src, dst, ssem, rsem, device_id=(rr, cc), device_id_type=MESH).start()

    def put(src, dst, ssem, rsem, rr, cc):
        me = jnp.logical_and(rr == r, cc == c)

        @pl.when(me)
        def _():
            pltpu.make_async_copy(src, dst, rsem).start()

        @pl.when(jnp.logical_not(me))
        def _():
            remote(src, dst, ssem, rsem, rr, cc)

    def wait_for(ref, sem):
        pltpu.make_async_copy(ref, ref, sem).wait()

    load_i = [pltpu.make_async_copy(starts_in, starts, s_sem.at[0]), pltpu.make_async_copy(sel_in, sel, s_sem.at[1])]
    for copy in load_i:
        copy.start()
    load_w = pltpu.make_async_copy(wf.at[:, 0], wf_v, w_sem)
    load_w.start()
    load_x = [pltpu.make_async_copy(m, raw.at[i], raw_sem.at[i]) for i, m in enumerate((s_in, t_in, q_in, z_in))]
    for copy in load_x:
        copy.start()
    for copy in load_i:
        copy.wait()
    window_of_block(starts, inv_v)
    ident = jnp.where(
        lax.broadcasted_iota(jnp.int32, (8, 128), 0) + rt * 8
        == lax.broadcasted_iota(jnp.int32, (8, 128), 1) + lt * 128, 1.0, 0.0).astype(F32)
    for k in range(NK):
        recv_a[16, k] = ident
    load_w.wait()
    permute_rows(sel, wf_v, send_a, r, c)
    move_inv = pltpu.make_async_copy(inv_v, inv, i_sem)
    move_inv.start()

    pl.semaphore_wait(barrier, 15 + NC - 1)

    for i in range(1, 16):
        rr = rem(r + i, 16)
        remote(send_a.at[div(rr, 2), rem(rr, 2)], recv_a.at[r], a_send, a_recv, rr, c)
    pltpu.make_async_copy(send_a.at[q, h], recv_a.at[r], a_recv).start()
    for i in (4, 5, 3, 2, 6, 1, 7):
        signal(ready, r, rem(c + i, NC))
    for copy in load_x:
        copy.wait()
    for i in range(4):
        for a in range(2):
            for b in range(NB):
                pltpu.make_async_copy(raw.at[i, a, :, b, :], xs.at[i, b, pl.ds(a * W, W)], x_sem).start()
    move_inv.wait()
    pl.semaphore_wait(ready, NC - 1)
    wait_for(recv_a.at[pl.ds(0, 16)], a_recv)

    place = recv_b.at[:, pl.ds(pl.multiple_of(rt * 8, 8), 8), pl.ds(pl.multiple_of(lt * 128, 128), 128)]
    for i in range(32):
        for k in range(NK):
            send_b[i, k] = recv_a[inv[k, i], k]
    for i in (4, 5, 3, 2, 6, 1, 7):
        cc = rem(c + i, NC)
        for b in range(NB):
            remote(send_b.at[cc + NC * b], place, b_send, b_recv, task_chip(b, h, cc) * 2 + h, cc)
    for i in range(1, NB):
        b = rem(task_b + i, NB)
        remote(send_b.at[c + NC * b], place, b_send, b_recv, task_chip(b, h, c) * 2 + h, c)
    put(send_b.at[c + NC * task_b], place, b_send, b_recv, task_chip(task_b, h, c) * 2 + h, c)

    def part(first, count):
        return pl.ds(pl.multiple_of(first, 64), count)

    mine, theirs = part(h * 128, 128), part((1 - h) * 128, 128)
    near, far = part(h * 128, 64), part(h * 128 + 64, 64)
    partner = r + 1 - 2 * h

    def slot_at(dx, dy):
        kk, bb = task_of(rem(x + dx, 4), rem(y + dy, 2), c)
        return kk * NB + bb

    own = kind * NB + task_b

    @pl.when(is_task)
    def _():
        wait_for(recv_b, b_recv)
        combo[...] = mm(split(mm(split(recv_b[0]), split(recv_b[1]))), split(recv_b[2]))
        pltpu.make_async_copy(combo.at[mine], colf.at[own, mine], c_recv.at[0]).start()
        remote(combo.at[theirs], colf.at[own, theirs], o_send, c_recv.at[0], partner, c)
        pltpu.make_async_copy(combo.at[theirs], colf.at[own, theirs], e_recv).start()

        @pl.when(kind == 0)
        def _():
            for p in range(2):
                rows = pl.ds(p * 128, 128)
                put(combo.at[rows], rowl.at[div(task_b, 2), rows], t_send, d_recv.at[div(task_b, 2), p],
                    c + NC * (rem(task_b, 2)), c)
                remote(combo.at[rows], rowl.at[div(task_b, 2), rows], t_send, d_recv.at[div(task_b, 2), p],
                       c + NC * (rem(task_b, 2)), c + 1 - 2 * rem(c, 2))

    left, right = rem(r + 12, 16), rem(r + 4, 16)
    across = x * 4 + (1 - y) * 2 + h

    def got(slot, rows, i):
        wait_for(colf.at[slot, rows], c_recv.at[i])

    def pass_on(slot, rows, i, rr):
        remote(colf.at[slot, rows], colf.at[slot, rows], c_send, c_recv.at[i], rr, c)

    def share(slot):
        remote(colf.at[slot, mine], colf.at[slot, mine], e_send, e_recv, partner, c)

    zd = rem(z + 4 - div(rem(r, NC), 2), 4)

    def got_row(a, p):
        wait_for(rowl.at[a, pl.ds(p * 128, 128)], d_recv.at[a, p])

    def pass_row(a, p):
        rows = pl.ds(p * 128, 128)
        remote(rowl.at[a, rows], rowl.at[a, rows], d_send, d_recv.at[a, p], r, rem(c + (2 if p == 0 else NC - 2), NC))

    got(own, mine, 0)
    pass_on(own, near, 1, right)
    pass_on(own, far, 4, left)
    pass_on(own, near, 5, across)
    pass_on(own, far, 2, right)
    pass_on(own, near, 3, left)
    pass_on(own, far, 6, across)

    @pl.when(is_task)
    def _():
        share(own)

    @pl.when(zd == 0)
    def _():
        for a in range(2):
            for p in range(2):
                got_row(a, p)
                pass_row(a, p)

    at_left, at_right, at_across = slot_at(3, 0), slot_at(1, 0), slot_at(0, 1)
    got(at_left, near, 1)
    pass_on(at_left, near, 7, right)
    pass_on(at_left, near, 9, across)
    got(at_right, far, 4)
    pass_on(at_right, far, 8, left)
    pass_on(at_right, far, 12, across)
    got(at_across, near, 5)
    pass_on(at_across, near, 11, left)
    got(at_across, far, 6)
    pass_on(at_across, far, 10, right)
    share(at_across)

    @pl.when(zd == 1)
    def _():
        for a in range(2):
            got_row(a, 0)
            pass_row(a, 0)

    @pl.when(zd == 3)
    def _():
        for a in range(2):
            got_row(a, 1)
            pass_row(a, 1)

    got(at_left, far, 2)
    share(at_left)
    got(at_right, near, 3)
    share(at_right)
    across_left, across_right = slot_at(3, 1), slot_at(1, 1)
    got(across_left, near, 9)
    pass_on(across_left, near, 13, right)
    got(across_right, far, 12)
    pass_on(across_right, far, 14, left)
    got(across_left, far, 10)
    share(across_left)
    got(across_right, near, 11)
    share(across_right)

    @pl.when(zd == 2)
    def _():
        for a in range(2):
            for p in range(2):
                got_row(a, p)
                pass_row(a, p)

    opposite, across_opposite = slot_at(2, 0), slot_at(2, 1)
    got(opposite, near, 7)
    got(opposite, far, 8)
    share(opposite)
    got(across_opposite, near, 13)
    got(across_opposite, far, 14)
    share(across_opposite)

    wait_for(xs, x_sem)
    wait_for(recv_a.at[pl.ds(0, 15)], a_send)
    wait_for(colf.at[:, theirs], e_recv)

    def halves(i, _):
        ch[i], cl[i] = split(colf[i])
        return 0

    def columns(b, _):
        for m in range(4):
            f = b if m == 2 else NB + b
            xs[m, b] = mm(split(xs[m, b]), (ch[f], cl[f]))
        return 0

    lax.fori_loop(0, NT, halves, 0)
    lax.fori_loop(0, NB, columns, 0)
    wait_for(colf.at[pl.ds(0, 7), mine], c_send)

    @pl.when(zd == 1)
    def _():
        got_row(0, 1)
        got_row(1, 1)

    @pl.when(zd == 3)
    def _():
        got_row(0, 0)
        got_row(1, 0)

    @pl.when(zd % 2 == 0)
    def _():
        wait_for(rowl, d_send)

    @pl.when(zd % 2 == 1)
    def _():
        wait_for(rowl.at[0], d_send)

    @pl.when(is_task)
    def _():
        wait_for(send_b.at[pl.ds(0, 31)], b_send)
        wait_for(combo.at[theirs], o_send)
        wait_for(colf.at[:, mine], e_send)

        @pl.when(kind == 0)
        def _():
            local = c + NC * (rem(task_b, 2)) == r

            @pl.when(local)
            def _():
                wait_for(rowl.at[0], t_send)

            @pl.when(jnp.logical_not(local))
            def _():
                wait_for(rowl, t_send)

    @pl.when(jnp.logical_not(is_task))
    def _():
        wait_for(send_b, b_send)
        wait_for(colf.at[pl.ds(0, 7), mine], e_send)


def comm_call(starts, sel, wf, s, t, q, z):
    dma = pltpu.SemaphoreType.DMA
    br, w, bc, _ = s.shape
    return pl.pallas_call(
        comm_kernel,
        out_shape=[
            pltpu.VMEM((br, W, W), F32), pltpu.VMEM((4, bc, br * w, w), F32),
        ],
        in_specs=[pl.BlockSpec(memory_space=pltpu.HBM)] * 7,
        out_specs=[VM, VM],
        scratch_shapes=[
            pltpu.VMEM((NT, W, W), F32), pltpu.VMEM((NT, W, W), BF), pltpu.VMEM((NT, W, W), BF),
            pltpu.VMEM(starts.shape, jnp.int32), pltpu.VMEM(sel.shape, jnp.int32),
            pltpu.VMEM((NK, 2, W, W), F32), pltpu.VMEM((NQ, 2, NK, 8, 128), F32),
            pltpu.VMEM((8, 128), jnp.int32), pltpu.SMEM((8, 128), jnp.int32),
            pltpu.VMEM((17, NK, 8, 128), F32), pltpu.VMEM((32, NK, 8, 128), F32),
            pltpu.VMEM((NK, W, W), F32), pltpu.VMEM((W, W), F32), pltpu.VMEM((4, br, w, bc, w), F32),
            pltpu.SemaphoreType.REGULAR, dma((2,)), dma, dma, dma((4,)), dma, dma, dma, dma, dma,
            dma, dma, dma((15,)), dma, dma, dma, dma, dma((2, 2)),
        ],
        compiler_params=pltpu.CompilerParams(has_side_effects=True, vmem_limit_bytes=24 * 1024 * 1024, collective_id=0),
        name="comm",
    )(*(pltpu.with_memory_space_constraint(v, pltpu.HBM) for v in (starts, sel, wf, s, t, q, z)))


def finish_kernel(xs, rowl, os, ot, oq, oz, obuf, rh, rl, out_sem):
    _, bc, rows, w = xs.shape
    br = rows // w
    outs = (os, ot, oq, oz)

    def store(src, m, a, b):
        pltpu.make_async_copy(src.at[m, b, pl.ds(a * w, w)], outs[m].at[a, :, b, :], out_sem).start()

    for b in range(bc):
        for m in range(2, 4):
            for a in range(br):
                store(xs, m, a, b)
    for a in range(br):
        rh[a], rl[a] = split(rowl[a].T)

    def row_blocks(b, _):
        for m in range(2):
            for a in range(br):
                part = pl.ds(a * w, w)
                obuf[m, b, part] = mm((rh[a], rl[a]), split(xs[m, b, part]))
        for m in range(2):
            for a in range(br):
                store(obuf, m, a, b)
        return 0

    lax.fori_loop(0, bc, row_blocks, 0)
    pltpu.make_async_copy(xs, xs, out_sem).wait()


def finish_call(shape, xs, rowl):
    br, w, bc, _ = shape
    return pl.pallas_call(
        finish_kernel,
        out_shape=[jax.ShapeDtypeStruct(shape, F32)] * 4,
        in_specs=[VM, VM],
        out_specs=[ANY] * 4,
        scratch_shapes=[
            pltpu.VMEM((2,) + xs.shape[1:], F32),
            pltpu.VMEM((br, w, w), BF), pltpu.VMEM((br, w, w), BF),
            pltpu.SemaphoreType.DMA,
        ],
        compiler_params=pltpu.CompilerParams(vmem_limit_bytes=24 * 1024 * 1024),
        name="finish",
    )(xs, rowl)


def shards(s, t, q, z, starts, sel, wf):
    rowl, xs = comm_call(starts, sel, wf, s, t, q, z)
    return finish_call(s.shape, xs, rowl)


def solution(mesh):
    spec = P(None, "row", None, "col")
    return jax.shard_map(
        shards,
        mesh=mesh,
        in_specs=(spec,) * 4 + (P(), P(), P(None, "row")),
        out_specs=(spec,) * 4,
        check_vma=False,
    )
```

time: 94.7 us -> 51.7 us (0.55)
  the two profiles are of different devices: /device:TPU:25 before, /device:TPU:65 now
where the time goes in v1:
time: 51.7 us; the launch traced here: 51.6 us
  Pallas kernels  51 us (99%)
  between operations  0.64 us (1%)
    pallas_call x1, Pallas kernels, comm_call(): pl.pallas_call(comm_kernel, out_shape=[pltpu.VMEM((br, W, W), F32), pltpu...  47.3 us
    pallas_call x1, Pallas kernels, finish_call(): pl.pallas_call(finish_kernel, out_shape=[jax.ShapeDtypeStruct(shape, F32)...  3.68 us

profile of v1, /device:TPU:65, one launch (start us, length us, event | category | flops | bytes accessed | tf_op | source)
XLA Modules:
  0.0 51.6 jit_solution(16775127363445452813)
XLA Ops:
  0.6 47.3 %comm.1 = (f32[2,256,256]{2,1,0:T(8,128)S(1)}, f32[4,4,512,256]{3,2,1,0:T(8,128)S(1)}) custom-call(s32[3,16]{1,0:T(4,128)} %starts_in.1, s32[3,16,256]{2,1,0:T(8,128)} %sel_in.1, f32[3,1,2,256,256]{4,3,2,1,0:T(8,128)} %wf.1, f32[2,256,4,256]{3,2,1,0:T(4,128)} %s_in.1, f32[2,256,4,256]{3,2,1,0:T(4,128)} %t_in.1, f32[2,256,4,256]{3,2,1,0:T(4,128)} %q_in.1, ...), custom_call_target="tpu_custom_call" | custom-call | tf_op jit(solution)/shard_map/comm/pallas_call | solution.py:362
  47.9 3.7 %finish.1 = (f32[2,256,4,256]{3,2,1,0:T(4,128)}, f32[2,256,4,256]{3,2,1,0:T(4,128)}, f32[2,256,4,256]{3,2,1,0:T(4,128)}, f32[2,256,4,256]{3,2,1,0:T(4,128)}) custom-call(f32[4,4,512,256]{3,2,1,0:T(8,128)S(1)} %get-tuple-element.6.xs, f32[2,256,256]{2,1,0:T(8,128)S(1)} %get-tuple-element.7.rowl), custom_call_target="tpu_custom_call" | custom-call | tf_op jit(solution)/shard_map/finish/pallas_call | solution.py:415

commit v2 on v1

--- a/solution.py
+++ b/solution.py
@@ -33,6 +33,7 @@
     return d(a[0], b[0]) + (d(a[0], b[1]) + d(a[1], b[0]))
 
 NT = 2 * NB
+SUB, DSUB = 2, 4
 
 
 def permute_rows(sel, wf, send, r, c):
@@ -85,7 +86,7 @@
 def comm_kernel(starts_in, sel_in, wf, s_in, t_in, q_in, z_in, rowl, xs, colf, ch, cl,
                 starts, sel, wf_v, send_a, inv_v, inv, recv_a, send_b, recv_b, combo, raw,
                 ready, s_sem, w_sem, i_sem, raw_sem, x_sem, a_send, a_recv, b_send, b_recv,
-                o_send, c_send, c_recv, e_send, e_recv, t_send, d_send, d_recv):
+                o_send, o_recv, c_send, c_recv, e_send, e_recv, t_send, d_send, d_recv):
     r, c = lax.axis_index("row"), lax.axis_index("col")
     x, y, h = div(r, 4), rem(div(r, 2), 2), rem(r, 2)
     q, z = div(r, 2), div(c, 2)
@@ -98,33 +99,33 @@
     def signal(sem, rr, cc):
         pl.semaphore_signal(sem, inc=1, device_id=(rr, cc), device_id_type=MESH)
 
-    for i in (4, 5, 3, 2, 6, 1, 7):
-        signal(barrier, r, rem(c + i, NC))
-    for i in range(1, 16):
-        signal(barrier, rem(r + i, 16), c)
-
-    def remote(src, dst, ssem, rsem, rr, cc):
-        pltpu.make_async_remote_copy(src, dst, ssem, rsem, device_id=(rr, cc), device_id_type=MESH).start()
-
-    def put(src, dst, ssem, rsem, rr, cc):
-        me = jnp.logical_and(rr == r, cc == c)
-
-        @pl.when(me)
-        def _():
-            pltpu.make_async_copy(src, dst, rsem).start()
-
-        @pl.when(jnp.logical_not(me))
-        def _():
-            remote(src, dst, ssem, rsem, rr, cc)
-
-    def wait_for(ref, sem):
-        pltpu.make_async_copy(ref, ref, sem).wait()
-
     load_i = [pltpu.make_async_copy(starts_in, starts, s_sem.at[0]), pltpu.make_async_copy(sel_in, sel, s_sem.at[1])]
     for copy in load_i:
         copy.start()
     load_w = pltpu.make_async_copy(wf.at[:, 0], wf_v, w_sem)
     load_w.start()
+    for i in (4, 5, 3, 2, 6, 1, 7):
+        signal(barrier, r, rem(c + i, NC))
+    for i in range(1, 16):
+        signal(barrier, rem(r + i, 16), c)
+
+    def remote(src, dst, ssem, rsem, rr, cc):
+        pltpu.make_async_remote_copy(src, dst, ssem, rsem, device_id=(rr, cc), device_id_type=MESH).start()
+
+    def put(src, dst, ssem, rsem, rr, cc):
+        me = jnp.logical_and(rr == r, cc == c)
+
+        @pl.when(me)
+        def _():
+            pltpu.make_async_copy(src, dst, rsem).start()
+
+        @pl.when(jnp.logical_not(me))
+        def _():
+            remote(src, dst, ssem, rsem, rr, cc)
+
+    def wait_for(ref, sem):
+        pltpu.make_async_copy(ref, ref, sem).wait()
+
     load_x = [pltpu.make_async_copy(m, raw.at[i], raw_sem.at[i]) for i, m in enumerate((s_in, t_in, q_in, z_in))]
     for copy in load_x:
         copy.start()
@@ -149,12 +150,6 @@
     pltpu.make_async_copy(send_a.at[q, h], recv_a.at[r], a_recv).start()
     for i in (4, 5, 3, 2, 6, 1, 7):
         signal(ready, r, rem(c + i, NC))
-    for copy in load_x:
-        copy.wait()
-    for i in range(4):
-        for a in range(2):
-            for b in range(NB):
-                pltpu.make_async_copy(raw.at[i, a, :, b, :], xs.at[i, b, pl.ds(a * W, W)], x_sem).start()
     move_inv.wait()
     pl.semaphore_wait(ready, NC - 1)
     wait_for(recv_a.at[pl.ds(0, 16)], a_recv)
@@ -172,44 +167,66 @@
         remote(send_b.at[c + NC * b], place, b_send, b_recv, task_chip(b, h, c) * 2 + h, c)
     put(send_b.at[c + NC * task_b], place, b_send, b_recv, task_chip(task_b, h, c) * 2 + h, c)
 
+    for copy in load_x:
+        copy.wait()
+    for i in range(4):
+        for a in range(2):
+            for b in range(NB):
+                pltpu.make_async_copy(raw.at[i, a, :, b, :], xs.at[i, b, pl.ds(a * W, W)], x_sem).start()
+
     def part(first, count):
-        return pl.ds(pl.multiple_of(first, 64), count)
+        return pl.ds(pl.multiple_of(first, 8), count)
 
     mine, theirs = part(h * 128, 128), part((1 - h) * 128, 128)
-    near, far = part(h * 128, 64), part(h * 128 + 64, 64)
+    near, far = 0, 1
+
+    def piece(side, u):
+        return part(h * 128 + side * 64 + u * (64 // SUB), 64 // SUB)
+
     partner = r + 1 - 2 * h
 
     def slot_at(dx, dy):
         kk, bb = task_of(rem(x + dx, 4), rem(y + dy, 2), c)
         return kk * NB + bb
 
+    def row_piece(p, u):
+        return pl.ds(p * 128 + u * (128 // DSUB), 128 // DSUB)
+
     own = kind * NB + task_b
 
     @pl.when(is_task)
     def _():
         wait_for(recv_b, b_recv)
         combo[...] = mm(split(mm(split(recv_b[0]), split(recv_b[1]))), split(recv_b[2]))
-        pltpu.make_async_copy(combo.at[mine], colf.at[own, mine], c_recv.at[0]).start()
-        remote(combo.at[theirs], colf.at[own, theirs], o_send, c_recv.at[0], partner, c)
+        pltpu.make_async_copy(combo.at[mine], colf.at[own, mine], o_recv).start()
+        remote(combo.at[theirs], colf.at[own, theirs], o_send, o_recv, partner, c)
         pltpu.make_async_copy(combo.at[theirs], colf.at[own, theirs], e_recv).start()
 
         @pl.when(kind == 0)
         def _():
-            for p in range(2):
-                rows = pl.ds(p * 128, 128)
-                put(combo.at[rows], rowl.at[div(task_b, 2), rows], t_send, d_recv.at[div(task_b, 2), p],
-                    c + NC * (rem(task_b, 2)), c)
-                remote(combo.at[rows], rowl.at[div(task_b, 2), rows], t_send, d_recv.at[div(task_b, 2), p],
-                       c + NC * (rem(task_b, 2)), c + 1 - 2 * rem(c, 2))
+            for u in range(DSUB):
+                for p in range(2):
+                    rows = row_piece(p, u)
+                    land, arrived = rowl.at[div(task_b, 2), rows], d_recv.at[div(task_b, 2), p, u]
+                    put(combo.at[rows], land, t_send, arrived, c + NC * rem(task_b, 2), c)
+                    remote(combo.at[rows], land, t_send, arrived, c + NC * rem(task_b, 2), c + 1 - 2 * rem(c, 2))
 
     left, right = rem(r + 12, 16), rem(r + 4, 16)
     across = x * 4 + (1 - y) * 2 + h
 
-    def got(slot, rows, i):
-        wait_for(colf.at[slot, rows], c_recv.at[i])
-
-    def pass_on(slot, rows, i, rr):
-        remote(colf.at[slot, rows], colf.at[slot, rows], c_send, c_recv.at[i], rr, c)
+    def got(slot, side, i):
+        for u in range(SUB):
+            wait_for(colf.at[slot, piece(side, u)], c_recv.at[i, u])
+
+    def send_piece(slot, side, u, i, rr):
+        rows = piece(side, u)
+        remote(colf.at[slot, rows], colf.at[slot, rows], c_send, c_recv.at[i, u], rr, c)
+
+    def relay(slot, side, i, *hops):
+        for u in range(SUB):
+            wait_for(colf.at[slot, piece(side, u)], c_recv.at[i, u])
+            for j, rr in hops:
+                send_piece(slot, side, u, j, rr)
 
     def share(slot):
         remote(colf.at[slot, mine], colf.at[slot, mine], e_send, e_recv, partner, c)
@@ -217,19 +234,27 @@
     zd = rem(z + 4 - div(rem(r, NC), 2), 4)
 
     def got_row(a, p):
-        wait_for(rowl.at[a, pl.ds(p * 128, 128)], d_recv.at[a, p])
-
-    def pass_row(a, p):
-        rows = pl.ds(p * 128, 128)
-        remote(rowl.at[a, rows], rowl.at[a, rows], d_send, d_recv.at[a, p], r, rem(c + (2 if p == 0 else NC - 2), NC))
-
-    got(own, mine, 0)
-    pass_on(own, near, 1, right)
-    pass_on(own, far, 4, left)
-    pass_on(own, near, 5, across)
-    pass_on(own, far, 2, right)
-    pass_on(own, near, 3, left)
-    pass_on(own, far, 6, across)
+        for u in range(DSUB):
+            wait_for(rowl.at[a, row_piece(p, u)], d_recv.at[a, p, u])
+
+    def relay_rows(*sides):
+        for u in range(DSUB):
+            for a in range(2):
+                for p in sides:
+                    rows = row_piece(p, u)
+                    wait_for(rowl.at[a, rows], d_recv.at[a, p, u])
+                    remote(rowl.at[a, rows], rowl.at[a, rows], d_send, d_recv.at[a, p, u],
+                           r, rem(c + (2 if p == 0 else NC - 2), NC))
+
+    wait_for(colf.at[own, mine], o_recv)
+    for u in range(SUB):
+        send_piece(own, near, u, 1, right)
+        send_piece(own, far, u, 4, left)
+        send_piece(own, near, u, 5, across)
+    for u in range(SUB):
+        send_piece(own, far, u, 6, across)
+        send_piece(own, far, u, 2, right)
+        send_piece(own, near, u, 3, left)
 
     @pl.when(is_task)
     def _():
@@ -237,57 +262,39 @@
 
     @pl.when(zd == 0)
     def _():
-        for a in range(2):
-            for p in range(2):
-                got_row(a, p)
-                pass_row(a, p)
+        relay_rows(0, 1)
 
     at_left, at_right, at_across = slot_at(3, 0), slot_at(1, 0), slot_at(0, 1)
-    got(at_left, near, 1)
-    pass_on(at_left, near, 7, right)
-    pass_on(at_left, near, 9, across)
-    got(at_right, far, 4)
-    pass_on(at_right, far, 8, left)
-    pass_on(at_right, far, 12, across)
-    got(at_across, near, 5)
-    pass_on(at_across, near, 11, left)
-    got(at_across, far, 6)
-    pass_on(at_across, far, 10, right)
+    relay(at_left, near, 1, (7, right), (9, across))
+    relay(at_right, far, 4, (8, left), (12, across))
+    relay(at_across, near, 5, (11, left))
+    relay(at_across, far, 6, (10, right))
     share(at_across)
 
     @pl.when(zd == 1)
     def _():
-        for a in range(2):
-            got_row(a, 0)
-            pass_row(a, 0)
+        relay_rows(0)
 
     @pl.when(zd == 3)
     def _():
-        for a in range(2):
-            got_row(a, 1)
-            pass_row(a, 1)
+        relay_rows(1)
 
     got(at_left, far, 2)
     share(at_left)
     got(at_right, near, 3)
     share(at_right)
     across_left, across_right = slot_at(3, 1), slot_at(1, 1)
-    got(across_left, near, 9)
-    pass_on(across_left, near, 13, right)
-    got(across_right, far, 12)
-    pass_on(across_right, far, 14, left)
+    relay(across_left, near, 9, (13, right))
+    relay(across_right, far, 12, (14, left))
+
+    @pl.when(zd == 2)
+    def _():
+        relay_rows(0, 1)
+
     got(across_left, far, 10)
     share(across_left)
     got(across_right, near, 11)
     share(across_right)
-
-    @pl.when(zd == 2)
-    def _():
-        for a in range(2):
-            for p in range(2):
-                got_row(a, p)
-                pass_row(a, p)
-
     opposite, across_opposite = slot_at(2, 0), slot_at(2, 1)
     got(opposite, near, 7)
     got(opposite, far, 8)
@@ -374,7 +381,7 @@
             pltpu.VMEM((17, NK, 8, 128), F32), pltpu.VMEM((32, NK, 8, 128), F32),
             pltpu.VMEM((NK, W, W), F32), pltpu.VMEM((W, W), F32), pltpu.VMEM((4, br, w, bc, w), F32),
             pltpu.SemaphoreType.REGULAR, dma((2,)), dma, dma, dma((4,)), dma, dma, dma, dma, dma,
-            dma, dma, dma((15,)), dma, dma, dma, dma, dma((2, 2)),
+            dma, dma, dma, dma((15, SUB)), dma, dma, dma, dma, dma((2, 2, DSUB)),
         ],
         compiler_params=pltpu.CompilerParams(has_side_effects=True, vmem_limit_bytes=24 * 1024 * 1024, collective_id=0),
         name="comm",

time: 51.7 us -> 47.4 us (0.917)
  the two profiles are of different devices: /device:TPU:65 before, /device:TPU:25 now
where the time goes in v2:
time: 47.4 us; the launch traced here: 46.6 us
  Pallas kernels  46 us (97%)
  between operations  0.64 us (1%)
    pallas_call x1, Pallas kernels, comm_call(): pl.pallas_call(comm_kernel, out_shape=[pltpu.VMEM((br, W, W), F32), pltpu...  42.3 us
    pallas_call x1, Pallas kernels, finish_call(): pl.pallas_call(finish_kernel, out_shape=[jax.ShapeDtypeStruct(shape, F32)...  3.67 us

profile of v2, /device:TPU:25, one launch (start us, length us, event | category | flops | bytes accessed | tf_op | source)
XLA Modules:
  0.0 46.6 jit_solution(3620401040953592942)
XLA Ops:
  0.6 42.3 %comm.1 = (f32[2,256,256]{2,1,0:T(8,128)S(1)}, f32[4,4,512,256]{3,2,1,0:T(8,128)S(1)}) custom-call(s32[3,16]{1,0:T(4,128)} %starts_in.1, s32[3,16,256]{2,1,0:T(8,128)} %sel_in.1, f32[3,1,2,256,256]{4,3,2,1,0:T(8,128)} %wf.1, f32[2,256,4,256]{3,2,1,0:T(4,128)} %s_in.1, f32[2,256,4,256]{3,2,1,0:T(4,128)} %t_in.1, f32[2,256,4,256]{3,2,1,0:T(4,128)} %q_in.1, ...), custom_call_target="tpu_custom_call" | custom-call | tf_op jit(solution)/shard_map/comm/pallas_call | solution.py:369
  43.0 3.7 %finish.1 = (f32[2,256,4,256]{3,2,1,0:T(4,128)}, f32[2,256,4,256]{3,2,1,0:T(4,128)}, f32[2,256,4,256]{3,2,1,0:T(4,128)}, f32[2,256,4,256]{3,2,1,0:T(4,128)}) custom-call(f32[4,4,512,256]{3,2,1,0:T(8,128)S(1)} %get-tuple-element.6.xs, f32[2,256,256]{2,1,0:T(8,128)S(1)} %get-tuple-element.7.rowl), custom_call_target="tpu_custom_call" | custom-call | tf_op jit(solution)/shard_map/finish/pallas_call | solution.py:422

commit v3 on v2

--- a/solution.py
+++ b/solution.py
@@ -198,10 +198,6 @@
     def _():
         wait_for(recv_b, b_recv)
         combo[...] = mm(split(mm(split(recv_b[0]), split(recv_b[1]))), split(recv_b[2]))
-        pltpu.make_async_copy(combo.at[mine], colf.at[own, mine], o_recv).start()
-        remote(combo.at[theirs], colf.at[own, theirs], o_send, o_recv, partner, c)
-        pltpu.make_async_copy(combo.at[theirs], colf.at[own, theirs], e_recv).start()
-
         @pl.when(kind == 0)
         def _():
             for u in range(DSUB):
@@ -210,6 +206,10 @@
                     land, arrived = rowl.at[div(task_b, 2), rows], d_recv.at[div(task_b, 2), p, u]
                     put(combo.at[rows], land, t_send, arrived, c + NC * rem(task_b, 2), c)
                     remote(combo.at[rows], land, t_send, arrived, c + NC * rem(task_b, 2), c + 1 - 2 * rem(c, 2))
+
+        pltpu.make_async_copy(combo.at[mine], colf.at[own, mine], o_recv).start()
+        remote(combo.at[theirs], colf.at[own, theirs], o_send, o_recv, partner, c)
+        pltpu.make_async_copy(combo.at[theirs], colf.at[own, theirs], e_recv).start()
 
     left, right = rem(r + 12, 16), rem(r + 4, 16)
     across = x * 4 + (1 - y) * 2 + h

time: 47.4 us -> 47 us (level)
  no operation moved by 1% of the time
where the time goes in v3:
time: 47 us; the launch traced here: 46.3 us
  Pallas kernels  45.6 us (97%)
  between operations  0.64 us (1%)
    pallas_call x1, Pallas kernels, comm_call(): pl.pallas_call(comm_kernel, out_shape=[pltpu.VMEM((br, W, W), F32), pltpu...  42 us
    pallas_call x1, Pallas kernels, finish_call(): pl.pallas_call(finish_kernel, out_shape=[jax.ShapeDtypeStruct(shape, F32)...  3.67 us

profile of v3, /device:TPU:25, one launch (start us, length us, event | category | flops | bytes accessed | tf_op | source)
XLA Modules:
  0.0 46.3 jit_solution(7878530652603322045)
XLA Ops:
  0.6 42.0 %comm.1 = (f32[2,256,256]{2,1,0:T(8,128)S(1)}, f32[4,4,512,256]{3,2,1,0:T(8,128)S(1)}) custom-call(s32[3,16]{1,0:T(4,128)} %starts_in.1, s32[3,16,256]{2,1,0:T(8,128)} %sel_in.1, f32[3,1,2,256,256]{4,3,2,1,0:T(8,128)} %wf.1, f32[2,256,4,256]{3,2,1,0:T(4,128)} %s_in.1, f32[2,256,4,256]{3,2,1,0:T(4,128)} %t_in.1, f32[2,256,4,256]{3,2,1,0:T(4,128)} %q_in.1, ...), custom_call_target="tpu_custom_call" | custom-call | tf_op jit(solution)/shard_map/comm/pallas_call | solution.py:369
  42.6 3.7 %finish.1 = (f32[2,256,4,256]{3,2,1,0:T(4,128)}, f32[2,256,4,256]{3,2,1,0:T(4,128)}, f32[2,256,4,256]{3,2,1,0:T(4,128)}, f32[2,256,4,256]{3,2,1,0:T(4,128)}) custom-call(f32[4,4,512,256]{3,2,1,0:T(8,128)S(1)} %get-tuple-element.6.xs, f32[2,256,256]{2,1,0:T(8,128)S(1)} %get-tuple-element.7.rowl), custom_call_target="tpu_custom_call" | custom-call | tf_op jit(solution)/shard_map/finish/pallas_call | solution.py:422
